TPU v7x, 32 devices: a whole 2x2x4 slice. The times are simulated.
32 devices in a mesh: groups: 2 (over y), seq: 4 (over z), head: 4 (over x, core).
Axes of the slice: x: 2, y: 2, z: 4, core: 2. Of those that a mesh axis runs over, the one named last changes fastest.
Arguments:
- query: bfloat16 [4, 8192], P('groups', 'head'), parts along dimension 0, may hold values from -170 to 170
- cache_keys: bfloat16 [4, 1024, 1024], P('groups', 'seq', 'head'), parts along dimension 0, may hold values from -6 to 6
- cache_values: bfloat16 [4, 1024, 1024], P('groups', 'seq', 'head'), parts along dimension 0, may hold values from -6 to 6
- lengths: int32 [4], P('groups'), parts along dimension 0, may hold values from 256 to 1024
- heavy: int32 [4, 2], P('groups'), parts along dimension 0, may hold values from 0 to 7, as said below
- acc_scores: float32 [4, 8], P('groups', 'seq'), parts along dimension 0, may hold values from 0.01 to 1
- refill_kv: bfloat16 [64, 2, 128, 128], P(('groups', 'seq', 'head')), parts along dimension 0, may hold values from -6 to 6
- refill_dest: int32 [64, 1], P(('groups', 'seq', 'head')), parts along dimension 0, may hold values from 0 to 3, as said below
- refill_req: int32 [64], P(('groups', 'seq', 'head')), parts along dimension 0, may hold values from 0 to 1
- refill_head: int32 [64], P(('groups', 'seq', 'head')), parts along dimension 0, may hold values from 0 to 1
Outputs:
- attn_out: bfloat16 [4, 8192], P('groups'), parts along dimension 0
- block_scores: float32 [4, 8], P('groups', 'seq'), parts along dimension 0
- recalled_kv: bfloat16 [64, 2, 128, 128], P(('groups', 'seq', 'head')), parts along dimension 0
- recall_scores: float32 [32, 2], P(('groups', 'seq', 'head')), parts along dimension 0
There are 2 independent parts, one for each index of `groups`. A program takes and returns all parts, laid end to end along the dimension named above; each array names one. Nothing has to cross between parts.
Inputs may be any that keep to these rules, and one draw needn't show every extreme that they name: `heavy`: the 2 block ids of one request are distinct. `refill_dest`: the block at position j of device (s, h) goes to owner (s + k) mod 4, with k fixed by h and j alone; among the 2 blocks of one device at most 2 name the same owner, and on every device 2 do.
All inputs are finite; a program needn't handle non-finite values.
Results may differ from a plain program's by a relative error of at most 0.0045.
Values may be sent and summed in bfloat16 or wider, within the bound.
A program may use at most 128 MiB of HBM per device.

v0:
```python
import functools
import math

import jax
import jax.numpy as jnp
from jax import lax
from jax.experimental import pallas as pl
from jax.experimental.pallas import tpu as pltpu
from jax.sharding import PartitionSpec as P

DH = 128
BLKTOK = 128
RECENT = 2
CHUNKS = 4
EARLY = 4
RELAYED = 4
LOW_PARITY = 1
SETTLE = (1, 0, 3, 2)
VMEM_OUT = 2**20
LANES = 128

NEG_BIG = -1e30


def round_up(value, step):
    return (value + step - 1) // step * step


def low_first(chunk):
    return chunk % 2 == LOW_PARITY


def kernel(
    dims,
    lengths_hbm,
    heavy_hbm,
    dest_hbm,
    req_hbm,
    head_hbm,
    acc_hbm,
    query_hbm,
    keys_hbm,
    values_hbm,
    refill_hbm,
    attn_ref,
    block_ref,
    recalled_ref,
    recall_ref,
    lengths_ref,
    heavy_ref,
    dest_ref,
    req_ref,
    head_ref,
    acc_ref,
    q_buf,
    k_buf,
    v_buf,
    own_kv,
    kv_buf,
    kept_kv,
    part_buf,
    stat_buf,
    mass_buf,
    load_sem,
    kv_send,
    kv_recv,
    part_send,
    part_recv,
    stat_send,
    stat_recv,
    attn_send,
    attn_recv,
    mass_send,
    mass_recv,
):
    n_seq, n_head, masks, chunks = dims
    requests, seq_local = k_buf.shape[0], k_buf.shape[1]
    kv_local = k_buf.shape[2] // DH
    heads_local = q_buf.shape[1] // DH
    per_group = heads_local // kv_local
    rows = requests * heads_local
    blocks_local = seq_local // BLKTOK
    held = own_kv.shape[0] // 2
    nheavy = heavy_ref.shape[1]
    stat_rows = stat_buf.shape[1]
    scale = 1.0 / math.sqrt(DH)

    me_seq = lax.axis_index("seq")
    me_head = lax.axis_index("head")

    def seq_peer(step):
        return lax.rem(me_seq + step, n_seq)

    def head_peer(step):
        return lax.rem(me_head + step, n_head)

    pairs = (
        (refill_hbm, own_kv),
        (query_hbm, q_buf),
        (keys_hbm, k_buf),
        (lengths_hbm, lengths_ref),
        (heavy_hbm, heavy_ref),
        (req_hbm, req_ref),
        (head_hbm, head_ref),
        (dest_hbm, dest_ref),
        (values_hbm, v_buf),
        (acc_hbm, acc_ref),
    )
    loads = [pltpu.make_async_copy(*pair, load_sem.at[i]) for i, pair in enumerate(pairs)]
    for load in loads:
        load.start()

    barrier = pltpu.get_barrier_semaphore()
    for step in range(1, n_seq):
        pl.semaphore_signal(barrier, inc=1, device_id={"seq": seq_peer(step)})
    for step in range(1, n_head):
        pl.semaphore_signal(barrier, inc=1, device_id={"head": head_peer(step)})

    loads[0].wait()

    stages = len(masks)
    pieces_per_chunk = 2 * held // chunks

    def mask_of(stage, chunk):
        return masks[stage] if low_first(chunk) else masks[stages - 1 - stage]

    def kv_copy(stage, chunk):
        mask = mask_of(stage, chunk)
        partner = me_seq + mask - 2 * mask * lax.rem(lax.div(me_seq, mask), 2)
        span = pl.ds(chunk * pieces_per_chunk, pieces_per_chunk)
        source = own_kv.at[span] if stage == 0 else kept_kv.at[stage - 1, span]
        return pltpu.make_async_remote_copy(
            src_ref=source,
            dst_ref=kv_buf.at[stage, span],
            send_sem=kv_send.at[stage, chunk],
            recv_sem=kv_recv.at[stage, chunk],
            device_id={"seq": partner},
        )

    kv_copies = {(i, c): kv_copy(i, c) for i in range(stages) for c in range(chunks)}

    def kv_settle(stage, chunk):
        mask = mask_of(stage, chunk)
        kv_copies[stage, chunk].wait_recv()
        for piece in range(chunk * pieces_per_chunk, (chunk + 1) * pieces_per_chunk):
            steps = steps_along[piece // 2]
            origin = me_seq
            if low_first(chunk):
                low = lax.rem(me_seq, mask)
                origin = me_seq - low + lax.rem(low - lax.rem(steps, mask) + mask, mask)
            old_bit = lax.rem(lax.div(me_seq, mask), 2)
            new_bit = lax.rem(lax.div(origin + steps, mask), 2)
            before = own_kv[piece] if stage == 0 else kept_kv[stage - 1, piece]
            after = jnp.where(old_bit == new_bit, before, kv_buf[stage, piece])
            if stage == stages - 1:
                recalled_ref[piece // 2, piece % 2] = after
            else:
                kept_kv[stage, piece] = after
        if stage < stages - 1:
            kv_copies[stage + 1, chunk].start()

    pl.semaphore_wait(barrier, n_seq + n_head - 2)

    for chunk in range(EARLY):
        kv_copies[0, chunk].start()

    for load in loads[1:]:
        load.wait()
    owners = [dest_ref[0, j] for j in range(held)]
    steps_along = [lax.rem(owners[j] - me_seq + n_seq, n_seq) for j in range(held)]

    q_rows = []
    for b in range(requests):
        line = q_buf[b : b + 1, :].astype(jnp.float32)
        for i in range(heads_local):
            q_rows.append(line[:, i * DH : (i + 1) * DH])
    q_all = jnp.concatenate(q_rows, axis=0).astype(jnp.bfloat16)

    contract = (((1,), (1,)), ((), ()))
    position = me_seq * seq_local + lax.broadcasted_iota(jnp.int32, (heads_local, seq_local), 1)
    token_block = lax.div(position, BLKTOK)
    cache_parts = []
    for b in range(requests):
        length = lengths_ref[b]
        keep = token_block >= lax.div(length - 1, BLKTOK) - (RECENT - 1)
        for n in range(nheavy):
            keep = keep | (token_block == heavy_ref[b, n])
        keep = keep & (position < length)
        seg_scores = []
        for g in range(kv_local):
            start = b * heads_local + g * per_group
            seg_scores.append(
                lax.dot_general(
                    q_all[start : start + per_group],
                    k_buf[b, :, g * DH : (g + 1) * DH],
                    contract,
                    preferred_element_type=jnp.float32,
                )
            )
        scores = jnp.concatenate(seg_scores, axis=0) * scale
        cache_parts.append(jnp.where(keep, scores, NEG_BIG))
    row_of = lax.broadcasted_iota(jnp.int32, (rows, BLKTOK), 0)
    segment_of = lax.div(row_of, per_group)
    unit_scores = []
    for u in range(held):
        member = segment_of == req_ref[u] * kv_local + head_ref[u]
        scores = (
            lax.dot_general(q_all, own_kv[2 * u], contract, preferred_element_type=jnp.float32)
            * scale
        )
        unit_scores.append(jnp.where(member, scores, NEG_BIG))

    cache_scores = jnp.concatenate(cache_parts, axis=0)
    best = jnp.max(cache_scores, axis=1, keepdims=True)
    for scores in unit_scores:
        best = jnp.maximum(best, jnp.max(scores, axis=1, keepdims=True))
    live = cache_scores > 0.5 * NEG_BIG
    cache_exp = jnp.where(live, jnp.exp(cache_scores - best), 0.0)
    block_sums = [
        jnp.sum(cache_exp[:, j * BLKTOK : (j + 1) * BLKTOK], axis=1, keepdims=True)
        for j in range(blocks_local)
    ]
    unit_exps = [
        jnp.where(scores > 0.5 * NEG_BIG, jnp.exp(scores - best), 0.0) for scores in unit_scores
    ]
    unit_sums = [jnp.sum(part, axis=1, keepdims=True) for part in unit_exps]
    total = functools.reduce(jnp.add, block_sums + unit_sums)

    lane = lax.broadcasted_iota(jnp.int32, (rows, LANES), 1)
    stats = jnp.zeros((rows, LANES), jnp.float32)
    for index, column in enumerate([best, total] + unit_sums + block_sums):
        stats = jnp.where(lane == index, column, stats)
    square = jnp.concatenate([stats, jnp.zeros((LANES - rows, LANES), jnp.float32)], axis=0)
    stat_buf[0] = square.T[:stat_rows]

    cache_exp = cache_exp.astype(jnp.bfloat16)
    outs = []
    for b in range(requests):
        for g in range(kv_local):
            start = b * heads_local + g * per_group
            outs.append(
                jnp.dot(
                    cache_exp[start : start + per_group],
                    v_buf[b, :, g * DH : (g + 1) * DH],
                    preferred_element_type=jnp.float32,
                )
            )
    accum = jnp.concatenate(outs, axis=0)
    for u in range(held):
        accum = accum + jnp.dot(
            unit_exps[u].astype(jnp.bfloat16), own_kv[2 * u + 1], preferred_element_type=jnp.float32
        )
    part_buf[0] = accum.astype(jnp.bfloat16)

    part_copies = []
    for step in range(1, n_seq):
        peer = seq_peer(step)
        for buf, send, recv in (
            (stat_buf, stat_send, stat_recv),
            (part_buf, part_send, part_recv),
        ):
            copy = pltpu.make_async_remote_copy(
                src_ref=buf.at[0],
                dst_ref=buf.at[step],
                send_sem=send.at[step],
                recv_sem=recv.at[step],
                device_id={"seq": peer},
            )
            copy.start()
            part_copies.append(copy)
    for chunk in range(EARLY, chunks):
        kv_copies[0, chunk].start()
    for chunk in SETTLE[:RELAYED]:
        kv_settle(0, chunk)
    for copy in part_copies:
        copy.wait_recv()

    row_best = stat_buf[0, 0:1]
    for step in range(1, n_seq):
        row_best = jnp.maximum(row_best, stat_buf[step, 0:1])
    valid = lax.broadcasted_iota(jnp.int32, (1, LANES), 1) < rows
    weights = []
    row_total = jnp.zeros((1, LANES), jnp.float32)
    for step in range(n_seq):
        weight = jnp.exp(stat_buf[step, 0:1] - row_best)
        weights.append(weight)
        row_total = row_total + weight * stat_buf[step, 1:2]
    inverse = jnp.where(valid, 1.0 / jnp.where(valid, row_total, 1.0), 0.0)
    factors = [weight * inverse for weight in weights]
    tall = jnp.concatenate(
        factors + [jnp.zeros((LANES - n_seq, LANES), jnp.float32)], axis=0
    ).T[:rows]
    joined = jnp.zeros((rows, DH), jnp.float32)
    for step in range(n_seq):
        joined = joined + part_buf[step].astype(jnp.float32) * tall[:, step : step + 1]

    width = heads_local * DH
    mine = pl.ds(pl.multiple_of(me_head * width, width), width)
    pieces = []
    for i in range(heads_local):
        pieces.append(
            jnp.concatenate(
                [
                    joined[b * heads_local + i : b * heads_local + i + 1]
                    for b in range(requests)
                ],
                axis=0,
            )
        )
    attn_ref[:, mine] = jnp.concatenate(pieces, axis=1).astype(jnp.bfloat16)

    tile_row = lax.broadcasted_iota(jnp.int32, (8, LANES), 0)
    tile_lane = lax.broadcasted_iota(jnp.int32, (8, LANES), 1)
    row_lane = lax.broadcasted_iota(jnp.int32, (1, LANES), 1)
    mass = jnp.zeros((8, LANES), jnp.float32)
    for j in range(blocks_local):
        share = stat_buf[0, 2 + held + j : 3 + held + j] * factors[0]
        for b in range(requests):
            inside = lax.div(row_lane, heads_local) == b
            value = jnp.sum(jnp.where(inside, share, 0.0), axis=1, keepdims=True)
            mass = jnp.where((tile_row == b) & (tile_lane == j), value, mass)
    mass_buf[0] = mass

    head_copies = []
    for step in range(1, n_head):
        peer = head_peer(step)
        for src, dst, send, recv in (
            (attn_ref.at[:, mine], attn_ref.at[:, mine], attn_send, attn_recv),
            (mass_buf.at[0], mass_buf.at[step], mass_send, mass_recv),
        ):
            copy = pltpu.make_async_remote_copy(
                src_ref=src,
                dst_ref=dst,
                send_sem=send.at[step],
                recv_sem=recv.at[step],
                device_id={"head": peer},
            )
            copy.start()
            head_copies.append(copy)

    recall = jnp.zeros((1, held), jnp.float32)
    held_lane = lax.broadcasted_iota(jnp.int32, (1, held), 1)
    for j in range(held):
        share = jnp.zeros((1, LANES), jnp.float32)
        for step in range(n_seq):
            term = stat_buf[step, 2 + j : 3 + j] * factors[step]
            share = share + jnp.where(steps_along[j] == step, term, 0.0)
        value = jnp.sum(share, axis=1, keepdims=True)
        recall = jnp.where(held_lane == j, value, recall)
    recall_ref[...] = recall

    for stage in range(stages):
        for chunk in SETTLE if stage else SETTLE[RELAYED:]:
            kv_settle(stage, chunk)

    for copy in head_copies:
        copy.wait_recv()
    mass = mass_buf[0]
    for step in range(1, n_head):
        mass = mass + mass_buf[step]
    block_ref[...] = acc_ref[...] + mass[:requests, :blocks_local]

    for copy in list(kv_copies.values()) + part_copies + head_copies:
        copy.wait_send()


def put_out(*refs):
    sources, targets, sems = refs[:4], refs[4:8], refs[8]
    copies = [
        pltpu.make_async_copy(source, target, sems.at[i])
        for i, (source, target) in enumerate(zip(sources, targets))
    ]
    for copy in copies:
        copy.start()
    for copy in copies:
        copy.wait()


def on_device(
    query,
    cache_keys,
    cache_values,
    lengths,
    heavy,
    acc_scores,
    refill_kv,
    refill_dest,
    refill_req,
    refill_head,
):
    n_seq = lax.axis_size("seq")
    n_head = lax.axis_size("head")
    requests = query.shape[0]
    rows = query.size // DH
    held = refill_kv.shape[0]
    masks = []
    while 2 ** len(masks) < n_seq:
        masks.append(2 ** len(masks))
    tiles = (2 * held,) + refill_kv.shape[2:]
    blocks_local = cache_keys.shape[1] // BLKTOK
    stat_rows = round_up(2 + held + blocks_local, 8)
    dma = pltpu.SemaphoreType.DMA
    hbm = pl.BlockSpec(memory_space=pltpu.HBM)
    vmem = pl.BlockSpec(memory_space=pltpu.VMEM)
    anywhere = pl.BlockSpec(memory_space=pl.ANY)
    results = pl.pallas_call(
        functools.partial(kernel, (n_seq, n_head, masks, CHUNKS)),
        out_shape=(
            pltpu.VMEM((requests, query.shape[1] * n_head), jnp.bfloat16),
            pltpu.VMEM(acc_scores.shape, jnp.float32),
            pltpu.VMEM(refill_kv.shape, jnp.bfloat16),
            pltpu.VMEM((1, held), jnp.float32),
        ),
        in_specs=[hbm] * 10,
        out_specs=(vmem,) * 4,
        scratch_shapes=[
            pltpu.SMEM(lengths.shape, jnp.int32),
            pltpu.SMEM(heavy.shape, jnp.int32),
            pltpu.SMEM((1, held), jnp.int32),
            pltpu.SMEM(refill_req.shape, jnp.int32),
            pltpu.SMEM(refill_head.shape, jnp.int32),
            pltpu.VMEM(acc_scores.shape, jnp.float32),
            pltpu.VMEM(query.shape, jnp.bfloat16),
            pltpu.VMEM(cache_keys.shape, jnp.bfloat16),
            pltpu.VMEM(cache_values.shape, jnp.bfloat16),
            pltpu.VMEM(tiles, jnp.bfloat16),
            pltpu.VMEM((len(masks),) + tiles, jnp.bfloat16),
            pltpu.VMEM((len(masks),) + tiles, jnp.bfloat16),
            pltpu.VMEM((n_seq, rows, DH), jnp.bfloat16),
            pltpu.VMEM((n_seq, stat_rows, LANES), jnp.float32),
            pltpu.VMEM((n_head, 8, LANES), jnp.float32),
            dma((10,)),
            dma((len(masks), CHUNKS)),
            dma((len(masks), CHUNKS)),
            dma((n_seq,)),
            dma((n_seq,)),
            dma((n_seq,)),
            dma((n_seq,)),
            dma((n_head,)),
            dma((n_head,)),
            dma((n_head,)),
            dma((n_head,)),
        ],
        compiler_params=pltpu.CompilerParams(
            collective_id=0, has_side_effects=True
        ),
    )(
        lengths,
        heavy,
        refill_dest.reshape(1, held),
        refill_req,
        refill_head,
        acc_scores,
        query,
        cache_keys,
        cache_values,
        refill_kv.reshape(tiles),
    )
    return pl.pallas_call(
        put_out,
        out_shape=tuple(jax.ShapeDtypeStruct(x.shape, x.dtype) for x in results),
        in_specs=[vmem] * 4,
        out_specs=(anywhere,) * 4,
        scratch_shapes=[dma((4,))],
        compiler_params=pltpu.CompilerParams(vmem_limit_bytes=VMEM_OUT),
    )(*results)


def solution(mesh):
    in_specs = (
        P("groups", "head"),
        P("groups", "seq", "head"),
        P("groups", "seq", "head"),
        P("groups"),
        P("groups", None),
        P("groups", "seq"),
        P(("groups", "seq", "head"), None, None, None),
        P(("groups", "seq", "head"), None),
        P(("groups", "seq", "head")),
        P(("groups", "seq", "head")),
    )
    out_specs = (
        P("groups", None),
        P("groups", "seq"),
        P(("groups", "seq", "head"), None, None, None),
        P(("groups", "seq", "head"), None),
    )
    return jax.shard_map(
        on_device, mesh=mesh, in_specs=in_specs, out_specs=out_specs, check_vma=False
    )
```

profile of v0, /device:TPU:0, one launch (start us, length us, event | category | flops | bytes accessed | tf_op | source)
XLA Modules:
  0.0 15.9 jit_solution(11448674125123893258)
XLA Ops:
  0.6 14.6 %shard_map.129 = (bf16[2,8192]{1,0:T(2,128)(2,1)S(1)}, f32[2,2]{1,0:T(2,128)S(1)}, bf16[2,2,128,128]{3,2,1,0:T(8,128)(2,1)S(1)}, f32[1,2]{1,0:T(1,128)S(1)}) custom-call(s32[2]{0:T(128)} %lengths_hbm.1, s32[2,2]{1,0:T(2,128)} %heavy_hbm.1, s32[1,2]{1,0:T(1,128)} %bitcast.3, s32[2]{0:T(128)} %req_hbm.1, s32[2]{0:T(128)} %head_hbm.1, f32[2,2]{1,0:T(2,128)} %acc_hbm.1, ...), custom_call_target="tpu_custom_call" | custom-call | tf_op jit(solution)/shard_map/pallas_call | solution.py:406
  15.2 0.7 %shard_map.130 = (bf16[2,8192]{1,0:T(2,128)(2,1)}, f32[2,2]{1,0:T(2,128)}, bf16[2,2,128,128]{3,2,1,0:T(8,128)(2,1)}, f32[1,2]{1,0:T(1,128)}) custom-call(bf16[2,8192]{1,0:T(2,128)(2,1)S(1)} %get-tuple-element.8.refs_0_, f32[2,2]{1,0:T(2,128)S(1)} %get-tuple-element.9.refs_1_, bf16[2,2,128,128]{3,2,1,0:T(8,128)(2,1)S(1)} %get-tuple-element.10.refs_2_, ...), custom_call_target="tpu_custom_call" | custom-call | tf_op jit(solution)/shard_map/pallas_call | solution.py:459
where the time goes:
time: 16.1 us; the launch traced here: 15.9 us
  Pallas kernels  15.3 us (95%)
  between operations  0.64 us (4%)
    pallas_call x1, Pallas kernels, on_device(): pl.pallas_call(functools.partial(kernel, (n_seq, n_head, masks, CHUNKS)),...  14.6 us
    pallas_call x1, Pallas kernels, on_device(): pl.pallas_call(put_out, out_shape=tuple((jax.ShapeDtypeStruct(x.shape, x....  0.71 us

commit v1 on v0

--- a/solution.py
+++ b/solution.py
@@ -12,22 +12,25 @@
 BLKTOK = 128
 RECENT = 2
 CHUNKS = 4
-EARLY = 4
+EARLY = 2
+EAGER = 2
+LOW_PARITY = 1
+ORDER = (1, 0, 3, 2)
+SETTLE = (1, 3, 0, 2)
 RELAYED = 4
-LOW_PARITY = 1
-SETTLE = (1, 0, 3, 2)
+LAST = (1, 3, 0, 2)
 VMEM_OUT = 2**20
 LANES = 128
 
 NEG_BIG = -1e30
 
 
-def round_up(value, step):
-    return (value + step - 1) // step * step
-
-
 def low_first(chunk):
     return chunk % 2 == LOW_PARITY
+
+
+def await_all(ref, sem):
+    pltpu.make_async_copy(ref, ref, sem.at[0]).wait()
 
 
 def kernel(
@@ -72,6 +75,8 @@
     attn_recv,
     mass_send,
     mass_recv,
+    seq_ready,
+    head_ready,
 ):
     n_seq, n_head, masks, chunks = dims
     requests, seq_local = k_buf.shape[0], k_buf.shape[1]
@@ -80,9 +85,10 @@
     per_group = heads_local // kv_local
     rows = requests * heads_local
     blocks_local = seq_local // BLKTOK
-    held = own_kv.shape[0] // 2
+    unit_rows = 2 * BLKTOK
+    held = own_kv.shape[0] // unit_rows
     nheavy = heavy_ref.shape[1]
-    stat_rows = stat_buf.shape[1]
+    per_line = LANES // rows
     scale = 1.0 / math.sqrt(DH)
 
     me_seq = lax.axis_index("seq")
@@ -111,30 +117,52 @@
         load.start()
 
     barrier = pltpu.get_barrier_semaphore()
-    for step in range(1, n_seq):
-        pl.semaphore_signal(barrier, inc=1, device_id={"seq": seq_peer(step)})
-    for step in range(1, n_head):
-        pl.semaphore_signal(barrier, inc=1, device_id={"head": head_peer(step)})
+    for axis, me, size in (("seq", me_seq, n_seq), ("head", me_head, n_head)):
+        for gap in range(1, size):
+
+            @pl.when(me + gap < size)
+            def _():
+                pl.semaphore_signal(barrier, inc=1, device_id={axis: me + gap})
+
+    @pl.when(me_seq + me_head > 0)
+    def _():
+        pl.semaphore_wait(barrier, me_seq + me_head)
+
+    for gap in range(1, n_seq):
+
+        @pl.when(me_seq >= gap)
+        def _():
+            pl.semaphore_signal(seq_ready.at[gap - 1], inc=1, device_id={"seq": me_seq - gap})
+
+    for gap in range(1, n_head):
+
+        @pl.when(me_head >= gap)
+        def _():
+            pl.semaphore_signal(head_ready, inc=1, device_id={"head": me_head - gap})
 
     loads[0].wait()
 
     stages = len(masks)
-    pieces_per_chunk = 2 * held // chunks
+    span_rows = own_kv.shape[0] // chunks
 
     def mask_of(stage, chunk):
         return masks[stage] if low_first(chunk) else masks[stages - 1 - stage]
 
+    def bit_of(place, mask):
+        return lax.rem(lax.div(place, mask), 2)
+
+    def held_at(stage):
+        return own_kv if stage == 0 else kept_kv.at[stage - 1]
+
     def kv_copy(stage, chunk):
         mask = mask_of(stage, chunk)
-        partner = me_seq + mask - 2 * mask * lax.rem(lax.div(me_seq, mask), 2)
-        span = pl.ds(chunk * pieces_per_chunk, pieces_per_chunk)
-        source = own_kv.at[span] if stage == 0 else kept_kv.at[stage - 1, span]
+        span = pl.ds(chunk * span_rows, span_rows)
         return pltpu.make_async_remote_copy(
-            src_ref=source,
+            src_ref=held_at(stage).at[span],
             dst_ref=kv_buf.at[stage, span],
-            send_sem=kv_send.at[stage, chunk],
+            send_sem=kv_send.at[0],
             recv_sem=kv_recv.at[stage, chunk],
-            device_id={"seq": partner},
+            device_id={"seq": me_seq + mask - 2 * mask * bit_of(me_seq, mask)},
         )
 
     kv_copies = {(i, c): kv_copy(i, c) for i in range(stages) for c in range(chunks)}
@@ -142,32 +170,45 @@
     def kv_settle(stage, chunk):
         mask = mask_of(stage, chunk)
         kv_copies[stage, chunk].wait_recv()
-        for piece in range(chunk * pieces_per_chunk, (chunk + 1) * pieces_per_chunk):
-            steps = steps_along[piece // 2]
+        first, last = chunk * span_rows, (chunk + 1) * span_rows
+        while first < last:
+            tile = first // BLKTOK
+            size = min(last, (tile + 1) * BLKTOK) - first
+            span = pl.ds(first, size)
+            steps = steps_along[tile // 2]
             origin = me_seq
             if low_first(chunk):
                 low = lax.rem(me_seq, mask)
                 origin = me_seq - low + lax.rem(low - lax.rem(steps, mask) + mask, mask)
-            old_bit = lax.rem(lax.div(me_seq, mask), 2)
-            new_bit = lax.rem(lax.div(origin + steps, mask), 2)
-            before = own_kv[piece] if stage == 0 else kept_kv[stage - 1, piece]
-            after = jnp.where(old_bit == new_bit, before, kv_buf[stage, piece])
+            stays = bit_of(me_seq, mask) == bit_of(origin + steps, mask)
+            after = jnp.where(stays, held_at(stage)[span], kv_buf[stage, span])
             if stage == stages - 1:
-                recalled_ref[piece // 2, piece % 2] = after
+                recalled_ref[tile // 2, tile % 2, pl.ds(first % BLKTOK, size)] = after
             else:
-                kept_kv[stage, piece] = after
+                kept_kv[stage, span] = after
+            first += size
         if stage < stages - 1:
             kv_copies[stage + 1, chunk].start()
 
-    pl.semaphore_wait(barrier, n_seq + n_head - 2)
-
-    for chunk in range(EARLY):
-        kv_copies[0, chunk].start()
+    def kv_start(chunk, upward):
+        @pl.when(bit_of(me_seq, mask_of(0, chunk)) == 1 - upward)
+        def _():
+            kv_copies[0, chunk].start()
+
+    eager = lax.rem(me_head, 2) < EAGER
+
+    @pl.when(eager)
+    def _():
+        for chunk in ORDER[:EARLY]:
+            kv_start(chunk, 0)
 
     for load in loads[1:]:
         load.wait()
     owners = [dest_ref[0, j] for j in range(held)]
     steps_along = [lax.rem(owners[j] - me_seq + n_seq, n_seq) for j in range(held)]
+
+    def tile_of(tile):
+        return pl.ds(tile * BLKTOK, BLKTOK)
 
     q_rows = []
     for b in range(requests):
@@ -205,7 +246,7 @@
     for u in range(held):
         member = segment_of == req_ref[u] * kv_local + head_ref[u]
         scores = (
-            lax.dot_general(q_all, own_kv[2 * u], contract, preferred_element_type=jnp.float32)
+            lax.dot_general(q_all, own_kv[tile_of(2 * u)], contract, preferred_element_type=jnp.float32)
             * scale
         )
         unit_scores.append(jnp.where(member, scores, NEG_BIG))
@@ -226,12 +267,15 @@
     unit_sums = [jnp.sum(part, axis=1, keepdims=True) for part in unit_exps]
     total = functools.reduce(jnp.add, block_sums + unit_sums)
 
-    lane = lax.broadcasted_iota(jnp.int32, (rows, LANES), 1)
-    stats = jnp.zeros((rows, LANES), jnp.float32)
-    for index, column in enumerate([best, total] + unit_sums + block_sums):
-        stats = jnp.where(lane == index, column, stats)
-    square = jnp.concatenate([stats, jnp.zeros((LANES - rows, LANES), jnp.float32)], axis=0)
-    stat_buf[0] = square.T[:stat_rows]
+    columns = [best, total] + unit_sums
+    lines = stat_buf.shape[1]
+    columns += [jnp.zeros_like(best)] * (lines * per_line - len(columns))
+    lane = lax.broadcasted_iota(jnp.int32, (LANES, LANES), 1)
+    square = jnp.zeros((LANES, LANES), jnp.float32)
+    for line in range(lines):
+        column = jnp.concatenate(columns[line * per_line : (line + 1) * per_line], axis=0)
+        square = jnp.where(lane == line, column, square)
+    stat_buf[0] = square.T[:lines]
 
     cache_exp = cache_exp.astype(jnp.bfloat16)
     outs = []
@@ -248,48 +292,74 @@
     accum = jnp.concatenate(outs, axis=0)
     for u in range(held):
         accum = accum + jnp.dot(
-            unit_exps[u].astype(jnp.bfloat16), own_kv[2 * u + 1], preferred_element_type=jnp.float32
+            unit_exps[u].astype(jnp.bfloat16), own_kv[tile_of(2 * u + 1)], preferred_element_type=jnp.float32
         )
     part_buf[0] = accum.astype(jnp.bfloat16)
 
-    part_copies = []
-    for step in range(1, n_seq):
-        peer = seq_peer(step)
+
+    def part_start(step):
         for buf, send, recv in (
             (stat_buf, stat_send, stat_recv),
             (part_buf, part_send, part_recv),
         ):
-            copy = pltpu.make_async_remote_copy(
+            pltpu.make_async_remote_copy(
                 src_ref=buf.at[0],
                 dst_ref=buf.at[step],
-                send_sem=send.at[step],
-                recv_sem=recv.at[step],
-                device_id={"seq": peer},
-            )
-            copy.start()
-            part_copies.append(copy)
-    for chunk in range(EARLY, chunks):
-        kv_copies[0, chunk].start()
+                send_sem=send.at[0],
+                recv_sem=recv.at[0],
+                device_id={"seq": seq_peer(step)},
+            ).start()
+
+    for gap in range(1, n_seq):
+
+        @pl.when(me_seq == gap)
+        def _():
+            part_start(n_seq - gap)
+
+    @pl.when(jnp.logical_not(eager))
+    def _():
+        for chunk in ORDER[:EARLY]:
+            kv_start(chunk, 0)
+
+    for chunk in ORDER[EARLY:]:
+        kv_start(chunk, 0)
+
+    for gap in reversed(range(1, n_seq)):
+
+        @pl.when(me_seq > gap)
+        def _():
+            part_start(n_seq - gap)
+
+    for gap in range(1, n_seq):
+
+        @pl.when(me_seq + gap < n_seq)
+        def _():
+            pl.semaphore_wait(seq_ready.at[gap - 1], 1)
+            part_start(gap)
+
+        for chunk in ORDER:
+            if mask_of(0, chunk) == gap:
+                kv_start(chunk, 1)
+
     for chunk in SETTLE[:RELAYED]:
         kv_settle(0, chunk)
-    for copy in part_copies:
-        copy.wait_recv()
-
-    row_best = stat_buf[0, 0:1]
-    for step in range(1, n_seq):
-        row_best = jnp.maximum(row_best, stat_buf[step, 0:1])
-    valid = lax.broadcasted_iota(jnp.int32, (1, LANES), 1) < rows
-    weights = []
-    row_total = jnp.zeros((1, LANES), jnp.float32)
-    for step in range(n_seq):
-        weight = jnp.exp(stat_buf[step, 0:1] - row_best)
-        weights.append(weight)
-        row_total = row_total + weight * stat_buf[step, 1:2]
+    await_all(stat_buf.at[pl.ds(1, n_seq - 1)], stat_recv)
+    await_all(part_buf.at[pl.ds(1, n_seq - 1)], part_recv)
+
+    def stat_of(index):
+        line = stat_buf[:, index // per_line, :]
+        shift = index % per_line * rows
+        return pltpu.roll(line, LANES - shift, 1) if shift else line
+
+    row_lane = lax.broadcasted_iota(jnp.int32, (n_seq, LANES), 1)
+    bests = stat_of(0)
+    weights = jnp.exp(bests - jnp.max(bests, axis=0, keepdims=True))
+    row_total = jnp.sum(weights * stat_of(1), axis=0, keepdims=True)
+    valid = row_lane[:1] < rows
     inverse = jnp.where(valid, 1.0 / jnp.where(valid, row_total, 1.0), 0.0)
-    factors = [weight * inverse for weight in weights]
-    tall = jnp.concatenate(
-        factors + [jnp.zeros((LANES - n_seq, LANES), jnp.float32)], axis=0
-    ).T[:rows]
+    factors = weights * inverse
+    fill = jnp.zeros((LANES - n_seq, LANES), jnp.float32)
+    tall = jnp.concatenate([factors, fill], axis=0).T[:rows]
     joined = jnp.zeros((rows, DH), jnp.float32)
     for step in range(n_seq):
         joined = joined + part_buf[step].astype(jnp.float32) * tall[:, step : step + 1]
@@ -311,57 +381,60 @@
 
     tile_row = lax.broadcasted_iota(jnp.int32, (8, LANES), 0)
     tile_lane = lax.broadcasted_iota(jnp.int32, (8, LANES), 1)
-    row_lane = lax.broadcasted_iota(jnp.int32, (1, LANES), 1)
     mass = jnp.zeros((8, LANES), jnp.float32)
     for j in range(blocks_local):
-        share = stat_buf[0, 2 + held + j : 3 + held + j] * factors[0]
+        share = block_sums[j] * tall[:, 0:1]
         for b in range(requests):
-            inside = lax.div(row_lane, heads_local) == b
-            value = jnp.sum(jnp.where(inside, share, 0.0), axis=1, keepdims=True)
+            of_request = share[b * heads_local : (b + 1) * heads_local]
+            value = jnp.sum(of_request, axis=0, keepdims=True)
             mass = jnp.where((tile_row == b) & (tile_lane == j), value, mass)
     mass_buf[0] = mass
 
-    head_copies = []
+    @pl.when(me_head < n_head - 1)
+    def _():
+        pl.semaphore_wait(head_ready, n_head - 1 - me_head)
+
     for step in range(1, n_head):
-        peer = head_peer(step)
         for src, dst, send, recv in (
             (attn_ref.at[:, mine], attn_ref.at[:, mine], attn_send, attn_recv),
             (mass_buf.at[0], mass_buf.at[step], mass_send, mass_recv),
         ):
-            copy = pltpu.make_async_remote_copy(
+            pltpu.make_async_remote_copy(
                 src_ref=src,
                 dst_ref=dst,
-                send_sem=send.at[step],
-                recv_sem=recv.at[step],
-                device_id={"head": peer},
-            )
-            copy.start()
-            head_copies.append(copy)
+                send_sem=send.at[0],
+                recv_sem=recv.at[0],
+                device_id={"head": head_peer(step)},
+            ).start()
 
     recall = jnp.zeros((1, held), jnp.float32)
     held_lane = lax.broadcasted_iota(jnp.int32, (1, held), 1)
+    slot = lax.broadcasted_iota(jnp.int32, (n_seq, LANES), 0)
     for j in range(held):
-        share = jnp.zeros((1, LANES), jnp.float32)
-        for step in range(n_seq):
-            term = stat_buf[step, 2 + j : 3 + j] * factors[step]
-            share = share + jnp.where(steps_along[j] == step, term, 0.0)
-        value = jnp.sum(share, axis=1, keepdims=True)
+        share = jnp.where(slot == steps_along[j], stat_of(2 + j) * factors, 0.0)
+        value = jnp.sum(jnp.sum(share, axis=0, keepdims=True), axis=1, keepdims=True)
         recall = jnp.where(held_lane == j, value, recall)
     recall_ref[...] = recall
 
-    for stage in range(stages):
-        for chunk in SETTLE if stage else SETTLE[RELAYED:]:
+    for chunk in SETTLE[RELAYED:]:
+        kv_settle(0, chunk)
+    for stage in range(1, stages):
+        for chunk in LAST:
             kv_settle(stage, chunk)
 
-    for copy in head_copies:
-        copy.wait_recv()
+    others = attn_ref.at[:, pl.ds(0, (n_head - 1) * width)]
+    await_all(others, attn_recv)
+    await_all(mass_buf.at[pl.ds(1, n_head - 1)], mass_recv)
     mass = mass_buf[0]
     for step in range(1, n_head):
         mass = mass + mass_buf[step]
     block_ref[...] = acc_ref[...] + mass[:requests, :blocks_local]
 
-    for copy in list(kv_copies.values()) + part_copies + head_copies:
-        copy.wait_send()
+    await_all(kv_buf, kv_send)
+    await_all(stat_buf.at[pl.ds(1, n_seq - 1)], stat_send)
+    await_all(part_buf.at[pl.ds(1, n_seq - 1)], part_send)
+    await_all(others, attn_send)
+    await_all(mass_buf.at[pl.ds(1, n_head - 1)], mass_send)
 
 
 def put_out(*refs):
@@ -396,9 +469,8 @@
     masks = []
     while 2 ** len(masks) < n_seq:
         masks.append(2 ** len(masks))
-    tiles = (2 * held,) + refill_kv.shape[2:]
-    blocks_local = cache_keys.shape[1] // BLKTOK
-    stat_rows = round_up(2 + held + blocks_local, 8)
+    tiles = (2 * held * BLKTOK, DH)
+    lines = -(-(2 + held) // (LANES // rows))
     dma = pltpu.SemaphoreType.DMA
     hbm = pl.BlockSpec(memory_space=pltpu.HBM)
     vmem = pl.BlockSpec(memory_space=pltpu.VMEM)
@@ -425,21 +497,16 @@
             pltpu.VMEM(cache_values.shape, jnp.bfloat16),
             pltpu.VMEM(tiles, jnp.bfloat16),
             pltpu.VMEM((len(masks),) + tiles, jnp.bfloat16),
-            pltpu.VMEM((len(masks),) + tiles, jnp.bfloat16),
+            pltpu.VMEM((max(len(masks) - 1, 1),) + tiles, jnp.bfloat16),
             pltpu.VMEM((n_seq, rows, DH), jnp.bfloat16),
-            pltpu.VMEM((n_seq, stat_rows, LANES), jnp.float32),
+            pltpu.VMEM((n_seq, lines, LANES), jnp.float32),
             pltpu.VMEM((n_head, 8, LANES), jnp.float32),
             dma((10,)),
+            dma((1,)),
             dma((len(masks), CHUNKS)),
-            dma((len(masks), CHUNKS)),
-            dma((n_seq,)),
-            dma((n_seq,)),
-            dma((n_seq,)),
-            dma((n_seq,)),
-            dma((n_head,)),
-            dma((n_head,)),
-            dma((n_head,)),
-            dma((n_head,)),
+            *[dma((1,))] * 8,
+            pltpu.SemaphoreType.REGULAR((n_seq - 1,)),
+            pltpu.SemaphoreType.REGULAR,
         ],
         compiler_params=pltpu.CompilerParams(
             collective_id=0, has_side_effects=True

time: 16.1 us -> 14.9 us (0.925)
  Pallas kernels: 15.3 us -> 14 us
    pallas_call x1, Pallas kernels: 14.6 us -> 13.3 us  [on_device(): pl.pallas_call(functools.partial(kernel, (n_seq, n_head, masks, CHUNKS)),...]
where the time goes in v1:
time: 14.9 us; the launch traced here: 14.6 us
  Pallas kernels  14 us (94%)
  between operations  0.64 us (4%)
    pallas_call x1, Pallas kernels, on_device(): pl.pallas_call(functools.partial(kernel, (n_seq, n_head, masks, CHUNKS)),...  13.3 us
    pallas_call x1, Pallas kernels, on_device(): pl.pallas_call(put_out, out_shape=tuple((jax.ShapeDtypeStruct(x.shape, x....  0.71 us

profile of v1, /device:TPU:0, one launch (start us, length us, event | category | flops | bytes accessed | tf_op | source)
XLA Modules:
  0.0 14.6 jit_solution(15722421170729976238)
XLA Ops:
  0.6 13.3 %shard_map.129 = (bf16[2,8192]{1,0:T(2,128)(2,1)S(1)}, f32[2,2]{1,0:T(2,128)S(1)}, bf16[2,2,128,128]{3,2,1,0:T(8,128)(2,1)S(1)}, f32[1,2]{1,0:T(1,128)S(1)}) custom-call(s32[2]{0:T(128)} %lengths_hbm.1, s32[2,2]{1,0:T(2,128)} %heavy_hbm.1, s32[1,2]{1,0:T(1,128)} %bitcast.3, s32[2]{0:T(128)} %req_hbm.1, s32[2]{0:T(128)} %head_hbm.1, f32[2,2]{1,0:T(2,128)} %acc_hbm.1, ...), custom_call_target="tpu_custom_call" | custom-call | tf_op jit(solution)/shard_map/pallas_call | solution.py:478
  13.9 0.7 %shard_map.130 = (bf16[2,8192]{1,0:T(2,128)(2,1)}, f32[2,2]{1,0:T(2,128)}, bf16[2,2,128,128]{3,2,1,0:T(8,128)(2,1)}, f32[1,2]{1,0:T(1,128)}) custom-call(bf16[2,8192]{1,0:T(2,128)(2,1)S(1)} %get-tuple-element.8.refs_0_, f32[2,2]{1,0:T(2,128)S(1)} %get-tuple-element.9.refs_1_, bf16[2,2,128,128]{3,2,1,0:T(8,128)(2,1)S(1)} %get-tuple-element.10.refs_2_, ...), custom_call_target="tpu_custom_call" | custom-call | tf_op jit(solution)/shard_map/pallas_call | solution.py:526

commit v2 on v1

--- a/solution.py
+++ b/solution.py
@@ -12,12 +12,12 @@
 BLKTOK = 128
 RECENT = 2
 CHUNKS = 4
-EARLY = 2
-EAGER = 2
+PLACES = 4
+EARLY = ((2, 2), (2, 2), (2, 2), (1, 4))
 LOW_PARITY = 1
 ORDER = (1, 0, 3, 2)
-SETTLE = (1, 3, 0, 2)
-RELAYED = 4
+BEFORE = ((), (1, 3, 0, 2), (1, 3, 0, 2), ())
+AFTER = ((0, 2, 1, 3), (), (), (1, 3, 0, 2))
 LAST = (1, 3, 0, 2)
 VMEM_OUT = 2**20
 LANES = 128
@@ -190,17 +190,23 @@
         if stage < stages - 1:
             kv_copies[stage + 1, chunk].start()
 
-    def kv_start(chunk, upward):
-        @pl.when(bit_of(me_seq, mask_of(0, chunk)) == 1 - upward)
-        def _():
-            kv_copies[0, chunk].start()
-
-    eager = lax.rem(me_head, 2) < EAGER
-
-    @pl.when(eager)
-    def _():
-        for chunk in ORDER[:EARLY]:
-            kv_start(chunk, 0)
+    place = lax.rem(me_seq, PLACES)
+    side = lax.rem(me_head, 2)
+
+    def kv_down(early):
+        for index, counts in enumerate(EARLY):
+            for half, count in enumerate(counts):
+
+                @pl.when((place == index) & (side == half))
+                def _():
+                    for chunk in ORDER[:count] if early else ORDER[count:]:
+                        mask = mask_of(0, chunk)
+                        if mask >= PLACES:
+                            pl.when(bit_of(me_seq, mask) == 1)(kv_copies[0, chunk].start)
+                        elif index & mask:
+                            kv_copies[0, chunk].start()
+
+    kv_down(True)
 
     for load in loads[1:]:
         load.wait()
@@ -316,13 +322,7 @@
         def _():
             part_start(n_seq - gap)
 
-    @pl.when(jnp.logical_not(eager))
-    def _():
-        for chunk in ORDER[:EARLY]:
-            kv_start(chunk, 0)
-
-    for chunk in ORDER[EARLY:]:
-        kv_start(chunk, 0)
+    kv_down(False)
 
     for gap in reversed(range(1, n_seq)):
 
@@ -337,12 +337,26 @@
             pl.semaphore_wait(seq_ready.at[gap - 1], 1)
             part_start(gap)
 
-        for chunk in ORDER:
-            if mask_of(0, chunk) == gap:
-                kv_start(chunk, 1)
-
-    for chunk in SETTLE[:RELAYED]:
-        kv_settle(0, chunk)
+        if gap in masks:
+
+            @pl.when(bit_of(me_seq, gap) == 0)
+            def _():
+                for chunk in ORDER:
+                    if mask_of(0, chunk) == gap:
+                        kv_copies[0, chunk].start()
+
+
+    def relay(orders):
+        for index, order in enumerate(orders):
+            if not order:
+                continue
+
+            @pl.when(place == index)
+            def _():
+                for chunk in order:
+                    kv_settle(0, chunk)
+
+    relay(BEFORE)
     await_all(stat_buf.at[pl.ds(1, n_seq - 1)], stat_recv)
     await_all(part_buf.at[pl.ds(1, n_seq - 1)], part_recv)
 
@@ -416,8 +430,7 @@
         recall = jnp.where(held_lane == j, value, recall)
     recall_ref[...] = recall
 
-    for chunk in SETTLE[RELAYED:]:
-        kv_settle(0, chunk)
+    relay(AFTER)
     for stage in range(1, stages):
         for chunk in LAST:
             kv_settle(stage, chunk)

time: 14.9 us -> 14.2 us (0.953)
  Pallas kernels: 14 us -> 13.4 us
    pallas_call x1, Pallas kernels: 13.3 us -> 12.7 us  [on_device(): pl.pallas_call(functools.partial(kernel, (n_seq, n_head, masks, CHUNKS)),...]
where the time goes in v2:
time: 14.2 us; the launch traced here: 14 us
  Pallas kernels  13.4 us (94%)
  between operations  0.64 us (5%)
    pallas_call x1, Pallas kernels, on_device(): pl.pallas_call(functools.partial(kernel, (n_seq, n_head, masks, CHUNKS)),...  12.7 us
    pallas_call x1, Pallas kernels, on_device(): pl.pallas_call(put_out, out_shape=tuple((jax.ShapeDtypeStruct(x.shape, x....  0.71 us

profile of v2, /device:TPU:0, one launch (start us, length us, event | category | flops | bytes accessed | tf_op | source)
XLA Modules:
  0.0 14.0 jit_solution(10176180832687338555)
XLA Ops:
  0.6 12.7 %shard_map.129 = (bf16[2,8192]{1,0:T(2,128)(2,1)S(1)}, f32[2,2]{1,0:T(2,128)S(1)}, bf16[2,2,128,128]{3,2,1,0:T(8,128)(2,1)S(1)}, f32[1,2]{1,0:T(1,128)S(1)}) custom-call(s32[2]{0:T(128)} %lengths_hbm.1, s32[2,2]{1,0:T(2,128)} %heavy_hbm.1, s32[1,2]{1,0:T(1,128)} %bitcast.3, s32[2]{0:T(128)} %req_hbm.1, s32[2]{0:T(128)} %head_hbm.1, f32[2,2]{1,0:T(2,128)} %acc_hbm.1, ...), custom_call_target="tpu_custom_call" | custom-call | tf_op jit(solution)/shard_map/pallas_call | solution.py:491
  13.3 0.7 %shard_map.130 = (bf16[2,8192]{1,0:T(2,128)(2,1)}, f32[2,2]{1,0:T(2,128)}, bf16[2,2,128,128]{3,2,1,0:T(8,128)(2,1)}, f32[1,2]{1,0:T(1,128)}) custom-call(bf16[2,8192]{1,0:T(2,128)(2,1)S(1)} %get-tuple-element.8.refs_0_, f32[2,2]{1,0:T(2,128)S(1)} %get-tuple-element.9.refs_1_, bf16[2,2,128,128]{3,2,1,0:T(8,128)(2,1)S(1)} %get-tuple-element.10.refs_2_, ...), custom_call_target="tpu_custom_call" | custom-call | tf_op jit(solution)/shard_map/pallas_call | solution.py:539
